TPU v7x, 128 devices: a whole 4x4x4 slice. The times are simulated.
128 devices in a mesh: dp: 1, model: 2 (over core), ctx: 64 (over z, y, x).
Axes of the slice: x: 4, y: 4, z: 4, core: 2. Of those that a mesh axis runs over, the one named last changes fastest.
Arguments:
- x_tokens: bfloat16 [4096, 7168], P(('dp', 'ctx'))
- positions: int32 [4096], P(('dp', 'ctx'))
- w_dq: bfloat16 [7168, 1536], replicated
- gain_q: float32 [1536], replicated
- w_uq: bfloat16 [1536, 8192], P(None, 'model')
- w_qr: bfloat16 [1536, 4096], P(None, 'model')
- w_dkv: bfloat16 [7168, 512], replicated
- gain_kv: float32 [512], replicated
- w_kr: bfloat16 [7168, 64], replicated
- w_uk: bfloat16 [512, 8192], P(None, 'model')
- w_uv: bfloat16 [512, 8192], P(None, 'model')
- w_out: bfloat16 [8192, 7168], P('model')
Outputs:
- output: bfloat16 [4096, 7168], P(('dp', 'ctx', 'model'))
All inputs are finite; a program needn't handle non-finite values.
Results may differ from a plain program's by a relative error of at most 0.00810006.
Values are sent between devices in bfloat16 or wider.
A program may use at most 1 GiB of HBM per device.

v0:
```python
import jax
import jax.numpy as jnp
from jax import lax
from jax.sharding import PartitionSpec as P

NORM_EPS = 1e-6
ROPE_BASE = 10000.0
NEG_BIG = -1e30


def rms_norm(hidden, gain):
    mean_sq = jnp.mean(hidden * hidden, axis=-1, keepdims=True)
    return (hidden * lax.rsqrt(mean_sq + NORM_EPS) * gain).astype(jnp.bfloat16)


def apply_rope(vals, positions):
    half_dim = vals.shape[-1] // 2
    inv_freq = ROPE_BASE ** (-(jnp.arange(half_dim, dtype=jnp.float32) * 2.0 / vals.shape[-1]))
    angles = positions.astype(jnp.float32)[:, None] * inv_freq[None, :]
    angles = angles.reshape((vals.shape[0],) + (1,) * (vals.ndim - 2) + (half_dim,))
    cos_ang = jnp.cos(angles)
    sin_ang = jnp.sin(angles)
    lower_half = vals[..., :half_dim]
    upper_half = vals[..., half_dim:]
    return jnp.concatenate([lower_half * cos_ang - upper_half * sin_ang, upper_half * cos_ang + lower_half * sin_ang], axis=-1)


def project(x_tokens, positions, w_dq, gain_q, w_uq, w_qr, w_dkv, gain_kv, w_kr):
    tok_rows = x_tokens.shape[0]
    rope_dim = w_kr.shape[1]
    heads_loc = w_qr.shape[1] // rope_dim
    c_q = rms_norm(jnp.dot(x_tokens, w_dq, preferred_element_type=jnp.float32), gain_q)
    q_nope = jnp.dot(c_q, w_uq, preferred_element_type=jnp.float32).astype(jnp.bfloat16).reshape(tok_rows, heads_loc, -1)
    q_rope = apply_rope(jnp.dot(c_q, w_qr, preferred_element_type=jnp.float32).reshape(tok_rows, heads_loc, rope_dim), positions).astype(jnp.bfloat16)
    c_kv = rms_norm(jnp.dot(x_tokens, w_dkv, preferred_element_type=jnp.float32), gain_kv)
    k_rope = apply_rope(jnp.dot(x_tokens, w_kr, preferred_element_type=jnp.float32), positions).astype(jnp.bfloat16)
    return q_nope, q_rope, jnp.concatenate([c_kv, k_rope], axis=-1)


def up_project(latent_blk, w_uk, w_uv, heads_loc):
    kv_rank = w_uk.shape[0]
    tok_rows = latent_blk.shape[0]
    c_blk = latent_blk[:, :kv_rank]
    keys_blk = jnp.dot(c_blk, w_uk, preferred_element_type=jnp.float32).astype(jnp.bfloat16).reshape(tok_rows, heads_loc, -1)
    vals_blk = jnp.dot(c_blk, w_uv, preferred_element_type=jnp.float32).astype(jnp.bfloat16).reshape(tok_rows, heads_loc, -1)
    return keys_blk, vals_blk, latent_blk[:, kv_rank:]


def merge_block(run_state, q_nope, q_rope, q_pos, keys_blk, vals_blk, kr_blk, k_pos):
    m_run, l_run, acc_run = run_state
    score_scale = (q_nope.shape[-1] + q_rope.shape[-1]) ** -0.5
    scores = (jnp.einsum('qhd,khd->qhk', q_nope, keys_blk, preferred_element_type=jnp.float32) + jnp.einsum('qhr,kr->qhk', q_rope, kr_blk, preferred_element_type=jnp.float32)) * score_scale
    allowed = (k_pos[None, :] <= q_pos[:, None])[:, None, :]
    scores = jnp.where(allowed, scores, NEG_BIG)
    m_new = jnp.maximum(m_run, jnp.max(scores, axis=-1))
    exp_scores = jnp.where(allowed, jnp.exp(scores - m_new[..., None]), 0.0)
    rescale = jnp.exp(m_run - m_new)
    l_new = rescale * l_run + jnp.sum(exp_scores, axis=-1)
    acc_new = rescale[..., None] * acc_run + jnp.einsum('qhk,khd->qhd', exp_scores.astype(jnp.bfloat16), vals_blk, preferred_element_type=jnp.float32)
    return m_new, l_new, acc_new


def solution(mesh):
    ctx_size = mesh.shape['ctx']
    shift_perm = [(src_dev, (src_dev + 1) % ctx_size) for src_dev in range(ctx_size)]

    def local(x_tokens, positions, w_dq, gain_q, w_uq, w_qr, w_dkv, gain_kv, w_kr, w_uk, w_uv, w_out):
        q_nope, q_rope, latent = project(x_tokens, positions, w_dq, gain_q, w_uq, w_qr, w_dkv, gain_kv, w_kr)
        tok_rows = q_nope.shape[0]
        heads_loc = q_nope.shape[1]
        v_dim = w_uv.shape[1] // heads_loc
        start_state = (jnp.full((tok_rows, heads_loc), NEG_BIG, jnp.float32), jnp.zeros((tok_rows, heads_loc), jnp.float32), jnp.zeros((tok_rows, heads_loc, v_dim), jnp.float32))
        keys_blk, vals_blk, kr_blk = up_project(latent, w_uk, w_uv, heads_loc)
        first_state = merge_block(start_state, q_nope, q_rope, positions, keys_blk, vals_blk, kr_blk, positions)

        def hop(hop_idx, carry):
            run_state, latent_blk, pos_blk = carry
            latent_blk = lax.ppermute(latent_blk, 'ctx', shift_perm)
            pos_blk = lax.ppermute(pos_blk, 'ctx', shift_perm)
            keys_in, vals_in, kr_in = up_project(latent_blk, w_uk, w_uv, heads_loc)
            run_state = merge_block(run_state, q_nope, q_rope, positions, keys_in, vals_in, kr_in, pos_blk)
            return run_state, latent_blk, pos_blk

        final_state = lax.fori_loop(1, ctx_size, hop, (first_state, latent, positions))[0]
        out_heads = (final_state[2] / final_state[1][..., None]).astype(jnp.bfloat16).reshape(tok_rows, heads_loc * v_dim)
        y_part = jnp.dot(out_heads, w_out, preferred_element_type=jnp.float32)
        return lax.psum_scatter(y_part, 'model', scatter_dimension=0, tiled=True).astype(jnp.bfloat16)

    in_specs = (P(('dp', 'ctx'), None), P(('dp', 'ctx')), P(), P(), P(None, 'model'), P(None, 'model'), P(), P(), P(), P(None, 'model'), P(None, 'model'), P('model', None))
    out_specs = P(('dp', 'ctx', 'model'), None)
    return jax.shard_map(local, mesh=mesh, in_specs=in_specs, out_specs=out_specs, check_vma=False)
```

profile of v0, /device:TPU:1, one launch (start us, length us, event | category | flops | bytes accessed | tf_op | source)
XLA Modules:
  0.0 1099.2 jit_solution(17038112694342279651)
XLA Ops:
  8.8 9.5 multiply_reduce_fusion
  38.7 953.1 %while.18 = (s32[]{:T(128)}, f32[64,32]{0,1:T(8,128)S(1)}, f32[64,32]{0,1:T(8,128)S(1)}, f32[64,32,128]{2,0,1:T(8,128)S(1)}, bf16[64,576]{1,0:T(8,128)(2,1)S(1)}...) while((s32[]{:T(128)}, f32[64,32]{0,1:T(8,128)S(1)}, ...), condition=%wide.region_7.8_spmd, body=%wide.region_4.7_spmd.sunk | while | flops 623124480 | bytes 34298080 | solution.py:84
  56.7 8.6 collective-permute-done.1
  71.7 8.6 collective-permute-done.1
  86.7 8.6 collective-permute-done.1
  101.7 8.6 collective-permute-done.1
  116.7 8.6 collective-permute-done.1
  131.6 8.6 collective-permute-done.1
  146.6 8.6 collective-permute-done.1
  161.6 8.6 collective-permute-done.1
  176.6 8.6 collective-permute-done.1
  191.6 8.6 collective-permute-done.1
  206.6 8.6 collective-permute-done.1
  221.5 8.6 collective-permute-done.1
  236.5 9.4 collective-permute-done.1
  252.2 9.7 collective-permute-done.1
  268.3 8.6 collective-permute-done.1
  283.3 8.6 collective-permute-done.1
  298.3 8.6 collective-permute-done.1
  313.2 8.6 collective-permute-done.1
  328.2 8.6 collective-permute-done.1
  343.2 8.6 collective-permute-done.1
  358.2 8.6 collective-permute-done.1
  373.2 8.6 collective-permute-done.1
  388.2 8.6 collective-permute-done.1
  403.1 8.6 collective-permute-done.1
  418.1 8.6 collective-permute-done.1
  433.1 8.6 collective-permute-done.1
  448.1 8.6 collective-permute-done.1
  463.1 9.5 collective-permute-done.1
  478.9 9.0 collective-permute-done.1
  494.3 8.6 collective-permute-done.1
  509.3 8.6 collective-permute-done.1
  524.3 8.6 collective-permute-done.1
  539.3 8.6 collective-permute-done.1
  554.2 8.6 collective-permute-done.1
  569.2 8.6 collective-permute-done.1
  584.2 8.6 collective-permute-done.1
  599.2 8.6 collective-permute-done.1
  614.2 8.6 collective-permute-done.1
  629.1 8.6 collective-permute-done.1
  674.1 9.5 collective-permute-done.1
  689.9 9.6 collective-permute-done.1
  795.8 8.6 collective-permute-done.1
  900.6 9.8 collective-permute-done.1
  916.8 9.0 collective-permute-done.1
  991.8 22.0 %fusion.28 = f32[64,7168]{1,0:T(8,128)} fusion(bf16[4096,7168]{1,0:T(8,128)(2,1)} %param.25, f32[64,32,128]{2,0,1:T(8,128)S(1)} %get-tuple-element.63, f32[64,32]{0,1:T(8,128)S(1)} %get-tuple-element.64), kind=kOutput, calls=%fused_computation.45 | convolution fusion | flops 3758620672 | bytes 61612032 | tf_op jit(solution)/shard_map/dot_general | solution.py:86
  1013.9 76.5 %reduce-scatter.2.cloned.1.call-done = f32[32,7168]{1,0:T(8,128)} async-done(((f32[64,7168]{1,0:T(8,128)}), f32[32,7168]{1,0:T(8,128)}) %reduce-scatter.2.cloned.1.call-update) | async-done | bytes 917520 | tf_op jit(solution)/shard_map/reduce_scatter | solution.py:87
  (1142 shorter events, 583.2 us)
Async XLA Ops:
  6.5 1083.8 %reduce-scatter.2.cloned.1.call-start = ((), (), s32[]{:S(2)}) async-start(), calls=%async_computation.1 | async-start | bytes 2752512 | tf_op jit(solution)/shard_map/reduce_scatter | solution.py:87
  38.9 11.6 %collective-permute-start = (bf16[64,576]{1,0:T(8,128)(2,1)S(1)}, bf16[64,576]{1,0:T(8,128)(2,1)S(1)}, u32[]{:S(2)}, u32[]{:S(2)}) collective-permute-start(bf16[64,576]{1,0:T(8,128)(2,1)S(1)} %get-tuple-element.220), channel_id=1, source_target_pairs={{0,1},{1,2},{2,3},{3,4},{4,5},{5,6},{6,7},{7,8},{8,9},{9,10},{10,1... | collective-permute-start | bytes 221192 | tf_op jit(solution)/shard_map/while/body/eval_jaxpr/ppermute | solution.py:78
  41.0 9.4 collective-permute-start.1
  56.6 8.9 collective-permute-start
  71.5 8.9 collective-permute-start
  86.5 8.9 collective-permute-start
  101.5 8.9 collective-permute-start
  116.5 8.9 collective-permute-start
  131.5 8.9 collective-permute-start
  146.5 8.9 collective-permute-start
  161.4 8.9 collective-permute-start
  176.4 8.9 collective-permute-start
  191.4 8.9 collective-permute-start
  206.4 8.9 collective-permute-start
  221.4 8.9 collective-permute-start
  236.3 9.6 collective-permute-start
  236.4 9.5 collective-permute-start.1
  252.1 10.0 collective-permute-start
  252.1 9.8 collective-permute-start.1
  268.1 8.9 collective-permute-start
  283.1 8.9 collective-permute-start
  298.1 8.9 collective-permute-start
  313.1 8.9 collective-permute-start
  328.1 8.9 collective-permute-start
  343.0 8.9 collective-permute-start
  358.0 8.9 collective-permute-start
  373.0 8.9 collective-permute-start
  388.0 8.9 collective-permute-start
  403.0 8.9 collective-permute-start
  432.9 8.9 collective-permute-start
  462.9 9.8 collective-permute-start
  463.0 9.6 collective-permute-start.1
  478.8 9.3 collective-permute-start
  478.8 9.1 collective-permute-start.1
  554.1 8.9 collective-permute-start
  599.0 8.9 collective-permute-start
  644.0 8.9 collective-permute-start
  673.9 9.7 collective-permute-start
  674.0 9.5 collective-permute-start.1
  689.7 9.9 collective-permute-start
  689.8 9.7 collective-permute-start.1
  735.7 8.9 collective-permute-start
  780.6 8.9 collective-permute-start
  825.5 8.9 collective-permute-start
  900.5 10.0 collective-permute-start
  900.5 9.9 collective-permute-start.1
  916.6 9.2 collective-permute-start
  916.7 9.1 collective-permute-start.1
  (153 other events, 1678.9 us)
Sparse Core Ops, SparseCore 0:
  1014.0 76.3 reduce-scatter.1
where the time goes:
time: 1100 us
  waiting for transfers between devices  626 us (57%)
  matrix products  407 us (37%)
  other arithmetic  27.9 us (3%)
  between operations  13.7 us (1%)
  starting transfers between devices  12.6 us (1%)
    ppermute x63, waiting for transfers between devices, hop(): pos_blk = lax.ppermute(pos_blk, 'ctx', shift_perm)  549 us
    dot_general x64, matrix products, up_project(): jnp.dot(c_blk, w_uk, preferred_element_type=jnp.float32)  192 us
    reduce_scatter x1, waiting for transfers between devices, local(): lax.psum_scatter(y_part, 'model', scatter_dimension=0, tiled=True)  76.5 us
    dot_general x64, matrix products, up_project(): jnp.dot(c_blk, w_uv, preferred_element_type=jnp.float32)  55.8 us
    dot_general x64, matrix products, merge_block(): jnp.einsum('qhk,khd->qhd', exp_scores.astype(jnp.bfloat16), vals_blk, pre...  49 us
    dot_general x64, matrix products, merge_block(): jnp.einsum('qhr,kr->qhk', q_rope, kr_blk, preferred_element_type=jnp.floa...  41.4 us
    dot_general x64, matrix products, merge_block(): jnp.einsum('qhd,khd->qhk', q_nope, keys_blk, preferred_element_type=jnp.f...  25.6 us
    dot_general x1, matrix products, local(): y_part = jnp.dot(out_heads, w_out, preferred_element_type=jnp.float32)  22 us
  transfers between devices with their start and end apart: 127, of which 64 were waited for; matrix products, arithmetic and copies ran while one was open for 0% of the time, Pallas kernels for 0%

commit v1 on v0

v1 whole, which is shorter than its diff:
```python
import math

import numpy as np
import jax
import jax.numpy as jnp
from jax import lax
from jax.experimental import pallas as pl
from jax.experimental.pallas import tpu as pltpu
from jax.sharding import PartitionSpec as P

NORM_EPS = 1e-6
ROPE_BASE = 10000.0
NEG_BIG = -1e30
MESH = pl.DeviceIdType.MESH
BF = jnp.bfloat16
F32 = jnp.float32

HIDDEN = 7168
Q_RANK = 1536
KV_RANK = 512
TOK = 64
SPAN = 32
HALF_SPAN = SPAN // 2
LANES = 128
QH = Q_RANK // 2
KH = KV_RANK // 2
BLK = 512
QB = 256
QK_DIM = 192
KEYS = 4096
ROWS_H = KEYS // 2
N_DOWN = HIDDEN // BLK
N_SIDE = N_DOWN // 2
N_OUT = HIDDEN // BLK
N_SLOTS = 8
N_EARLY = 4
N_TILES = 9
GROUP = 8
EXP_SCALE = QK_DIM ** -0.5 * math.log2(math.e)
LIMIT = 66 * 10 ** 6


def dot(a, b):
    return jnp.dot(a, b, preferred_element_type=F32)


def dot_dims(a, b, ca, cb):
    return lax.dot_general(a, b, (((ca,), (cb,)), ((), ())), preferred_element_type=F32)


def iota(shape, axis):
    return lax.broadcasted_iota(jnp.int32, shape, axis)


def dyn(i, width):
    return pl.ds(pl.multiple_of(i * width, math.gcd(width, BLK)), width)


class Ring:
    def __init__(self, blk, aux, p, right, left, ssem, rsem, row):
        prev, nxt, opp = (p + 3) % 4, (p + 1) % 4, (p + 2) % 4
        self.ssem, self.rsem, self.row = ssem, rsem, row
        self.sent = (
            (blk(p, 0), right, blk(prev, 0)),
            (blk(p, 1), left, blk(nxt, 1)),
            (aux(p), right, aux(prev)),
            (blk(p, 1), right, blk(prev, 1)),
            (blk(p, 0), left, blk(nxt, 0)),
            (aux(p), left, aux(nxt)),
            (blk(prev, 0), right, blk(opp, 0)),
            (blk(nxt, 1), left, blk(opp, 1)),
            (aux(prev), right, aux(opp)),
        )

    def copy(self, k, ref=None):
        ref = self.sent[k][0] if ref is None else ref
        return pltpu.make_async_remote_copy(ref, ref, self.ssem.at[self.row, k], self.rsem.at[self.row, k], device_id=self.sent[k][1], device_id_type=MESH)

    def recv(self, k):
        self.copy(k, self.sent[k][2]).wait_recv()

    def start_own(self):
        for k in range(6):
            self.copy(k).start()

    def forward(self):
        for k in range(3):
            self.recv(k)
            self.copy(k + 6).start()

    def recv_near(self):
        for k in range(3, 6):
            self.recv(k)

    def recv_far(self):
        for k in range(6, 9):
            self.recv(k)

    def wait_sends(self):
        for k in range(9):
            self.copy(k).wait_send()


def kernel(x_h, pos, inv, wdq, wdkv, wkr, gq, gkv, wuq, wqr, wuk, wuv, wout, y_ref,
           x_v, wkr_v, wbuf, h0, h1, hkr, tabs, stat, stat_rx, cq, lat, kr, pt,
           uq_v, qr_v, uk_v, uv_v, kcat, vbuf, qt, s_buf, m_s, l_s, acc_s, o_v, og, ysend, ykeep, yrecv,
           dsem, isem, osem, ssem, rsem, dssem, drsem, psem, assem, arsem, yssem, yrsem):
    c = lax.axis_index("ctx")
    m = lax.axis_index("model")
    x, y, z = c % 4, (c // 4) % 4, c // 16
    s, d = c // GROUP, c % GROUP
    first = m == 0
    sib = {"ctx": c, "model": 1 - m}
    pa, pb = jnp.where(first, z, y), jnp.where(first, y, z)
    sa, sb = jnp.where(first, 16, 4), jnp.where(first, 4, 16)
    yp = y % 2

    def at(idx):
        return {"ctx": idx, "model": m}

    def near(p, stride):
        return at(c + ((p + 1) % 4 - p) * stride), at(c + ((p + 3) % 4 - p) * stride)

    (xr, xl), (ar, al), (br, bl) = near(x, 1), near(pa, sa), near(pb, sb)
    ypair = at(c + 4 - 8 * yp)
    peers = [at(c - d + (d + k) % GROUP) for k in range(1, GROUP)]

    def down_copies(k):
        src = dyn(k, BLK)
        side, dst = k // N_SIDE, dyn(k % N_SIDE, BLK)
        q0 = pl.multiple_of(m * QH, LANES)
        return (
            pltpu.make_async_copy(wdq.at[src, pl.ds(q0, BLK)], wbuf.at[2 * side, dst], dsem.at[0, k]),
            pltpu.make_async_copy(wdq.at[src, pl.ds(pl.multiple_of(q0 + BLK, LANES), QB)], wbuf.at[2 * side + 1, dst, pl.ds(0, QB)], dsem.at[1, k]),
            pltpu.make_async_copy(wdkv.at[src, dyn(m, KH)], wbuf.at[2 * side + 1, dst, pl.ds(QB, KH)], dsem.at[2, k]),
        )

    def start_down(k, _):
        for cp in down_copies(k):
            cp.start()
        return 0

    def out_copy(j):
        return pltpu.make_async_copy(wout.at[:, dyn(j, BLK)], wbuf.at[lax.rem(j, N_SLOTS)], osem.at[lax.rem(j, N_SLOTS)])

    ins = [
        pltpu.make_async_copy(a, b, isem.at[i])
        for i, (a, b) in enumerate((
            (x_h, x_v), (wkr, wkr_v), (wuq.at[:, dyn(d, BLK)], uq_v), (wqr.at[:, dyn(d, QB)], qr_v),
            (wuk.at[:, dyn(d, BLK)], uk_v), (wuv.at[:, dyn(d, BLK)], uv_v),
        ))
    ]
    for cp in ins[:2]:
        cp.start()
    lax.fori_loop(0, N_DOWN, start_down, 0)
    for cp in ins[2:]:
        cp.start()
    for j in range(N_EARLY, N_SLOTS):
        out_copy(j).start()

    sem = pltpu.get_barrier_semaphore()
    greet = peers + [ar, al, br, bl, sib]
    for dev in greet:
        pl.semaphore_signal(sem, inc=1, device_id=dev, device_id_type=MESH)

    ang = inv[...] * pos[...].astype(F32)
    cos_f, sin_f = jnp.cos(ang), jnp.sin(ang)
    tabs[...] = jnp.transpose(jnp.concatenate([cos_f, cos_f, -sin_f, sin_f], axis=0))
    cs = jnp.transpose(jnp.concatenate([cos_f, sin_f], axis=0))

    def pack(v):
        return jnp.concatenate([v[:HALF_SPAN], v[HALF_SPAN:]], axis=-1)

    pt[m, yp, x] = pack(jnp.where(first, cs[:SPAN], cs[SPAN:]))

    h0[...] = jnp.zeros_like(h0)
    h1[...] = jnp.zeros_like(h1)
    hkr[...] = jnp.zeros_like(hkr)
    for cp in ins[:2]:
        cp.wait()

    def down(k, _):
        for cp in down_copies(k):
            cp.wait()
        side, rows = k // N_SIDE, dyn(k % N_SIDE, BLK)
        xb = x_v[:, dyn(k, BLK)]
        h0[...] += dot(xb, wbuf[2 * side, rows])
        h1[...] += dot(xb, wbuf[2 * side + 1, rows])
        hkr[...] += dot_dims(xb, wkr_v[:, dyn(k, BLK)], 1, 1)
        return 0

    lax.fori_loop(0, N_DOWN, down, 0)
    for j in range(N_EARLY):
        out_copy(j).start()

    h_q = jnp.concatenate([h0[...], h1[:, :QB]], axis=-1)
    h_kv = h1[:, QB:]
    own_q = jnp.sum(h_q * h_q, axis=-1, keepdims=True)
    own_kv = jnp.sum(h_kv * h_kv, axis=-1, keepdims=True)
    stat[...] = jnp.where(iota((TOK, LANES), 1) < TOK, own_q, own_kv)
    pl.semaphore_wait(sem, len(greet))
    st = pltpu.make_async_remote_copy(stat, stat_rx, psem.at[0], psem.at[1], device_id=sib, device_id_type=MESH)
    st.start()

    k_raw = hkr[...]
    swapped = jnp.concatenate([k_raw[:, SPAN:], k_raw[:, :SPAN]], axis=-1)
    k_rot = k_raw * tabs[:, :TOK] + swapped * tabs[:, TOK:]
    kr[m, pa, pb, x] = pack(jnp.where(first, k_rot[:SPAN], k_rot[SPAN:])).astype(BF)

    st.wait()
    tot_q = own_q + stat_rx[:, :1]
    tot_kv = own_kv + stat_rx[:, TOK:TOK + 1]
    nq, nk = QH // LANES, KH // LANES
    g_q = jnp.concatenate([gq[pl.ds(nq * m + i, 1), :] for i in range(nq)], axis=-1)
    g_kv = jnp.concatenate([gkv[pl.ds(nk * m + i, 1), :] for i in range(nk)], axis=-1)
    c_q = (h_q * lax.rsqrt(tot_q / Q_RANK + NORM_EPS) * g_q).astype(BF)
    c_kv = (h_kv * lax.rsqrt(tot_kv / KV_RANK + NORM_EPS) * g_kv).astype(BF)
    for half in range(2):
        lat[m, half, pa, pb, x] = c_kv[SPAN * half:SPAN * half + SPAN]
        cq[m, half, yp, x] = c_q[SPAN * half:SPAN * half + SPAN]

    def share(ref, k):
        return pltpu.make_async_remote_copy(ref, ref, dssem.at[k], drsem.at[k], device_id=sib, device_id_type=MESH)

    def row_ring(b, row):
        return Ring(lambda p, h: lat.at[m, h, p, b], lambda p: kr.at[m, p, b], pa, ar, al, ssem, rsem, row)

    r1 = Ring(lambda p, h: lat.at[m, h, pa, pb, p], lambda p: kr.at[m, pa, pb, p], x, xr, xl, ssem, rsem, 0)
    r2 = Ring(lambda p, h: lat.at[m, h, pa, p], lambda p: kr.at[m, pa, p], pb, br, bl, ssem, rsem, 1)
    rq = Ring(lambda p, h: cq.at[m, h, :, p], lambda p: pt.at[m, :, p], x, xr, xl, ssem, rsem, 2)
    r3 = [row_ring((pb + k) % 4, 3 + k) for k in range(4)]
    nxt, prev, opp = (pa + 1) % 4, (pa + 3) % 4, (pa + 2) % 4

    def pair_copies(par):
        return [
            pltpu.make_async_remote_copy(ref, ref, psem.at[2 + i], psem.at[4 + i], device_id=ypair, device_id_type=MESH)
            for i, ref in enumerate((cq.at[m, :, par, x], pt.at[m, par, x]))
        ]

    def shares(core, planes):
        refs = [cq.at[core], pt.at[core]]
        for p in planes:
            refs += [lat.at[core, :, p], kr.at[core, p]]
        return [share(ref, k) for k, ref in enumerate(refs)]

    mine = shares(m, (pa, prev, nxt, opp))

    r1.start_own()
    for cp in pair_copies(yp):
        cp.start()
    r1.forward()
    r1.recv_near()
    r1.recv_far()
    r2.start_own()
    r3[0].start_own()
    for cp in pair_copies(1 - yp):
        cp.wait_recv()
    rq.start_own()
    r2.forward()
    r2.recv_near()
    r3[1].start_own()
    r3[3].start_own()
    r3[0].forward()
    rq.forward()
    r2.recv_far()
    r3[2].start_own()
    for cp in mine[2:4]:
        cp.start()
    rq.recv_near()
    rq.recv_far()
    for cp in mine[:2]:
        cp.start()
    r3[1].forward()
    r3[3].forward()
    r3[2].forward()
    for r in r3:
        r.recv_near()
    for cp in mine[4:8]:
        cp.start()

    theirs = shares(1 - m, (0, 0, 0, 0))
    for cp in theirs[:2]:
        cp.wait_recv()
    for cp in ins[2:4]:
        cp.wait()
    t = pt[...].reshape(2 * LANES, LANES)
    grp = iota((2 * LANES, LANES), 1) // SPAN

    def both(shift):
        parts = []
        for extra in (0, TOK):
            v = pltpu.roll(t, (shift + extra) % LANES, 1) if shift + extra else t
            r = v
            for g in range(1, 4):
                r = jnp.where(grp == g, pltpu.roll(v, SPAN * g, 1), r)
            parts.append(r.reshape(HALF_SPAN, HALF_SPAN, LANES))
        return jnp.concatenate(parts, axis=1).reshape(BLK, LANES)

    lower = iota((BLK, LANES), 1) % TOK < SPAN
    cos_t = both(0)
    sin_t = both(LANES - SPAN)
    sin_t = jnp.where(lower, -sin_t, sin_t)
    c0, c1 = cq[0].reshape(BLK, QH), cq[1].reshape(BLK, QH)
    for p in range(2):
        wide, thin = slice(QB * p, QB * p + QB), slice(LANES * p, LANES * p + LANES)
        qn = dot(c0, uq_v[:QH, wide]) + dot(c1, uq_v[QH:, wide])
        qr = dot(c0, qr_v[:QH, thin]) + dot(c1, qr_v[QH:, thin])
        rot = jnp.where(lower, pltpu.roll(qr, LANES - SPAN, 1), pltpu.roll(qr, SPAN, 1))
        qn_t = jnp.transpose(qn).astype(BF)
        qr_t = jnp.transpose(qr * cos_t + rot * sin_t).astype(BF)
        for a in range(2):
            qt[2 * p + a, :LANES, :] = qn_t[LANES * a:LANES * a + LANES]
            qt[2 * p + a, LANES:QK_DIM, :] = qr_t[TOK * a:TOK * a + TOK]

    for r in r3:
        r.recv_far()
    for cp in mine[8:]:
        cp.start()
    for cp in ins[4:]:
        cp.wait()
    for cp in theirs[2:]:
        cp.wait_recv()

    for half in range(2):
        if half == 0:
            k2 = kr[0].reshape(ROWS_H // 2, LANES).astype(F32)
        else:
            k2 = jnp.concatenate([kr[1, :, zz].reshape(QB, LANES) for zz in range(4)], axis=0).astype(F32)
        lo = k2.reshape(TOK, HALF_SPAN, LANES)[:, :, :TOK]
        hi = pltpu.roll(k2, TOK, 1).reshape(TOK, HALF_SPAN, LANES)[:, :, :TOK]
        k3 = jnp.concatenate([lo, hi], axis=1).astype(BF).reshape(ROWS_H, TOK)
        for a in range(2):
            kcat[a, ROWS_H * half:ROWS_H * half + ROWS_H, LANES:QK_DIM] = k3

    nlow = s // 2 + 1

    def place(i):
        low = i < nlow
        b = jnp.where(low, i, i - nlow)
        return low, jnp.where(low, 0, 1), b, jnp.where(b < 4, b, 11 - b)

    def attn_sends(p):
        return [
            pltpu.make_async_remote_copy(
                o_v.at[:, (d + k) % GROUP, :, dyn(p, QB)], og.at[:, :, dyn(2 * d + p, QB)],
                assem.at[p, k - 1], arsem.at[p, k - 1], device_id=peers[k - 1], device_id_type=MESH)
            for k in range(1, GROUP)
        ]

    def pair(p, _):
        pc = dyn(p, QB)

        def up(i, _):
            half, zz = i // 4, i % 4
            a0 = lat[0, half, zz].reshape(BLK, KH)
            a1 = lat[1, half, :, zz].reshape(BLK, KH)
            rows = dyn(i, BLK)
            kn = (dot(a0, uk_v[:KH, pc]) + dot(a1, uk_v[KH:, pc])).astype(BF)
            kcat[0, rows, :LANES] = kn[:, :LANES]
            kcat[1, rows, :LANES] = kn[:, LANES:]
            vbuf[rows, :] = (dot(a0, uv_v[:KH, pc]) + dot(a1, uv_v[KH:, pc])).astype(BF)
            return 0

        lax.fori_loop(0, 8, up, 0)
        m_s[...] = jnp.full(m_s.shape, NEG_BIG, F32)
        l_s[...] = jnp.zeros_like(l_s)
        acc_s[...] = jnp.zeros_like(acc_s)

        def scores(i, a):
            _, qb, _, kb = place(i)
            return dot(kcat[a, dyn(kb, BLK), :QK_DIM], qt[2 * p + a, :, dyn(qb, QB)])

        for a in range(2):
            s_buf[a] = scores(0, a)

        def tile(i, _):
            low, qb, b, kb = place(i)

            @pl.when(b == jnp.where(low, s // 2, 7 - s // 2))
            def _():
                r = iota((BLK, 1), 0)
                cc = iota((1, QB), 1)
                k_idx = BLK * b + jnp.where(b < 4, r, (15 - r // SPAN) * SPAN + r % SPAN)
                q_idx = jnp.where(low, QB * s + cc, SPAN * (LANES - 1 - GROUP * s - cc // SPAN) + cc % SPAN)
                allowed = k_idx <= q_idx
                for a in range(2):
                    s_buf[a] = jnp.where(allowed, s_buf[a], NEG_BIG)

            after = jnp.minimum(i + 1, N_TILES - 1)
            for a in range(2):
                sc = s_buf[a]
                m_old = m_s[a, qb, :1, :]
                m_new = jnp.maximum(m_old, jnp.max(sc, axis=0, keepdims=True))
                e = jnp.exp2((sc - m_new) * EXP_SCALE)
                alpha = jnp.exp2((m_old - m_new) * EXP_SCALE)
                l_s[a, qb, :1, :] = l_s[a, qb, :1, :] * alpha + jnp.sum(e, axis=0, keepdims=True)
                s_buf[a] = scores(after, a)
                pv = dot_dims(vbuf[dyn(kb, BLK), LANES * a:LANES * a + LANES], e.astype(BF), 0, 0)
                acc_s[a, qb] = acc_s[a, qb] * alpha + pv
                m_s[a, qb, :1, :] = m_new
            return 0

        lax.fori_loop(0, N_TILES, tile, 0)
        for a in range(2):
            for qb in range(2):
                ot = acc_s[a, qb] / l_s[a, qb, :1, :]
                o_v[qb, :, :, dyn(2 * p + a, LANES)] = jnp.transpose(ot).astype(BF).reshape(GROUP, SPAN, LANES)
        for cp in attn_sends(p):
            cp.start()
        return 0

    lax.fori_loop(0, 2, pair, 0)
    og[:, :, dyn(d, BLK)] = o_v[:, d]

    for r in [r1, r2, rq] + r3:
        r.wait_sends()
    for cp in pair_copies(yp) + mine:
        cp.wait_send()
    for p in range(2):
        for cp in attn_sends(p):
            cp.wait()

    def y_copy(j):
        return pltpu.make_async_remote_copy(ysend.at[j], yrecv.at[j], yssem.at[j], yrsem.at[j], device_id=sib, device_id_type=MESH)

    def finish(j):
        y_copy(j).wait()
        y_ref[:, dyn(j, BLK)] = (ykeep[j] + yrecv[j]).astype(BF)

    def out_step(j, _):
        out_copy(j).wait()
        acc = dot(og[...].reshape(TOK, KEYS), wbuf[lax.rem(j, N_SLOTS)])
        ykeep[j] = jnp.where(first, acc[:SPAN], acc[SPAN:])
        ysend[j] = jnp.where(first, acc[SPAN:], acc[:SPAN])
        y_copy(j).start()

        @pl.when(j + N_SLOTS < N_OUT)
        def _():
            out_copy(j + N_SLOTS).start()

        @pl.when(j > 0)
        def _():
            finish(j - 1)
        return 0

    lax.fori_loop(0, N_OUT, out_step, 0)
    finish(N_OUT - 1)


def fused(x, pos, inv, wdq, wdkv, wkr, gq, gkv, wuq, wqr, wuk, wuv, wout):
    vm = pl.BlockSpec(memory_space=pltpu.VMEM)
    hbm = pl.BlockSpec(memory_space=pl.ANY)
    v, dma = pltpu.VMEM, pltpu.SemaphoreType.DMA
    state = v((2, 2, 8, QB), F32)
    part = v((N_OUT, SPAN, BLK), F32)
    return pl.pallas_call(
        kernel,
        name="mla_prefill",
        out_shape=jax.ShapeDtypeStruct((SPAN, HIDDEN), BF),
        in_specs=[hbm, vm, vm, hbm, hbm, hbm, vm, vm] + [hbm] * 5,
        out_specs=vm,
        scratch_shapes=[
            v((TOK, HIDDEN), BF), v((TOK, HIDDEN), BF), v((N_SLOTS, KEYS, BLK), BF),
            v((TOK, BLK), F32), v((TOK, BLK), F32), v((TOK, TOK), F32), v((TOK, LANES), F32), v((TOK, LANES), F32), v((TOK, LANES), F32),
            v((2, 2, 2, 4, SPAN, QH), BF), v((2, 2, 4, 4, 4, SPAN, KH), BF), v((2, 4, 4, 4, HALF_SPAN, LANES), BF), v((2, 2, 4, HALF_SPAN, LANES), F32),
            v((Q_RANK, BLK), BF), v((Q_RANK, QB), BF), v((KV_RANK, BLK), BF), v((KV_RANK, BLK), BF),
            v((2, KEYS, QB), BF), v((KEYS, QB), BF), v((4, QK_DIM, BLK), BF), v((2, BLK, QB), F32),
            state, state, v((2, 2, LANES, QB), F32), v((2, GROUP, SPAN, BLK), BF), v((2, SPAN, KEYS), BF), part, part, part,
            dma((3, N_DOWN)), dma((6,)), dma((N_SLOTS,)), dma((7, 9)), dma((7, 9)), dma((10,)), dma((10,)), dma((6,)),
            dma((2, 7)), dma((2, 7)), dma((N_OUT,)), dma((N_OUT,)),
        ],
        compiler_params=pltpu.CompilerParams(collective_id=0, has_side_effects=True, vmem_limit_bytes=LIMIT),
    )(x, pos, inv, wdq, wdkv, wkr, gq, gkv, wuq, wqr, wuk, wuv, wout)


def solution(mesh):
    freq = ROPE_BASE ** (-np.arange(SPAN) * 2.0 / TOK)
    inv = np.repeat(freq.astype(np.float32)[:, None], TOK, axis=1)

    def local(x_tokens, positions, w_dq, gain_q, w_uq, w_qr, w_dkv, gain_kv, w_kr, w_uk, w_uv, w_out):
        return fused(x_tokens, positions[None], inv, w_dq, w_dkv, w_kr.T, gain_q.reshape(-1, LANES), gain_kv.reshape(-1, LANES), w_uq, w_qr, w_uk, w_uv, w_out)

    in_specs = (P(('dp', 'ctx'), None), P(('dp', 'ctx')), P(), P(), P(None, 'model'), P(None, 'model'), P(), P(), P(), P(None, 'model'), P(None, 'model'), P('model', None))
    out_specs = P(('dp', 'ctx', 'model'), None)
    return jax.shard_map(local, mesh=mesh, in_specs=in_specs, out_specs=out_specs, check_vma=False)
```

time: 1100 us -> 79.8 us (0.07)
  waiting for transfers between devices: 626 us -> 0 us
  matrix products: 407 us -> 0 us
  Pallas kernels: 0 us -> 77.8 us
  other arithmetic: 27.9 us -> 0 us
  between operations: 13.7 us -> 0.01 us
  starting transfers between devices: 12.6 us -> 0 us
    ppermute x126 -> x0, waiting for transfers between devices: 550 us -> none  [the longest x63 549 us: hop(): pos_blk = lax.ppermute(pos_blk, 'ctx', shift_perm)]
    dot_general x326 -> x0, matrix products: 407 us -> none  [the longest x64 192 us: up_project(): jnp.dot(c_blk, w_uk, preferred_element_type=jnp.float32)]
    pallas_call x0 -> x1, Pallas kernels: none -> 77.8 us  [fused(): pl.pallas_call(kernel, name='mla_prefill', out_shape=jax.ShapeDtypeStruct...]
    reduce_scatter x1 -> x0, waiting for transfers between devices: 76.5 us -> none  [local(): lax.psum_scatter(y_part, 'model', scatter_dimension=0, tiled=True)]
    reduce_sum x64 -> x0, other arithmetic: 16.5 us -> none  [merge_block(): l_new = rescale * l_run + jnp.sum(exp_scores, axis=-1)]
    ppermute x126 -> x0, starting transfers between devices: 12.6 us -> none  [the longest x63 6.74 us: hop(): latent_blk = lax.ppermute(latent_blk, 'ctx', shift_perm)]
  transfers between devices with their start and end apart: 127 -> 0, of which waited for: 64 -> 0; matrix products, arithmetic and copies ran while one was open for 0% -> 0% of each run, Pallas kernels for 0% -> 0%
where the time goes in v1:
time: 79.8 us; the launch traced here: 79.6 us
  Pallas kernels  77.8 us (97%)
  local copies, waits for them, and re-layouts  1.82 us (2%)
    pallas_call x1, Pallas kernels, fused(): pl.pallas_call(kernel, name='mla_prefill', out_shape=jax.ShapeDtypeStruct...  77.8 us
    unnamed x1, local copies, waits for them, and re-layouts  1.82 us

profile of v1, /device:TPU:1, one launch (start us, length us, event | category | flops | bytes accessed | tf_op | source)
XLA Modules:
  0.0 79.6 jit_solution(8318883191915643375)
XLA Ops:
  0.0 77.8 %mla_prefill.1 = bf16[32,7168]{1,0:T(8,128)(2,1)} custom-call(bf16[64,7168]{1,0:T(8,128)(2,1)} %x_h.1, s32[1,64]{1,0:T(1,128)} %bitcast.7, f32[32,64]{1,0:T(8,128)} %constant.2.clone.inv, bf16[7168,1536]{1,0:T(8,128)(2,1)} %wdq.1, bf16[7168,512]{1,0:T(8,128)(2,1)} %wdkv.1, bf16[64,7168]{1,0:T(8,128)(2,1)} %bitcast.4, f32[12,128]{1,0:T(8,128)} %bitcast.5, ...), custom_call_target="tpu_custom_call" | custom-call | tf_op jit(solution)/shard_map/mla_prefill/pallas_call | solution.py:456
  77.8 1.8 %copy.15 = bf16[32,7168]{1,0:T(8,128)(2,1)} copy(bf16[32,7168]{1,0:T(8,128)(2,1)} %mla_prefill.1) | data formatting | bytes 917504

commit v2 on v1

--- a/solution.py
+++ b/solution.py
@@ -30,10 +30,8 @@
 KEYS = 4096
 ROWS_H = KEYS // 2
 N_DOWN = HIDDEN // BLK
-N_SIDE = N_DOWN // 2
 N_OUT = HIDDEN // BLK
-N_SLOTS = 8
-N_EARLY = 4
+N_SLOTS = 16
 N_TILES = 9
 GROUP = 8
 EXP_SCALE = QK_DIM ** -0.5 * math.log2(math.e)
@@ -54,6 +52,31 @@
 
 def dyn(i, width):
     return pl.ds(pl.multiple_of(i * width, math.gcd(width, BLK)), width)
+
+
+class Direct:
+    def __init__(self, blk, aux, p, devs, ssem, rsem, row):
+        self.ssem, self.rsem, self.row = ssem, rsem, row
+        self.sent = []
+        for off, dev in zip((1, 3, 2), devs):
+            src = (p - off + 4) % 4
+            self.sent += [(blk(p, 0), dev, blk(src, 0)), (blk(p, 1), dev, blk(src, 1)), (aux(p), dev, aux(src))]
+
+    def copy(self, k, ref=None):
+        ref = self.sent[k][0] if ref is None else ref
+        return pltpu.make_async_remote_copy(ref, ref, self.ssem.at[self.row, k], self.rsem.at[self.row, k], device_id=self.sent[k][1], device_id_type=MESH)
+
+    def start_own(self):
+        for k in range(9):
+            self.copy(k).start()
+
+    def recv_all(self):
+        for k in range(9):
+            self.copy(k, self.sent[k][2]).wait_recv()
+
+    def wait_sends(self):
+        for k in range(9):
+            self.copy(k).wait_send()
 
 
 class Ring:
@@ -83,8 +106,8 @@
         for k in range(6):
             self.copy(k).start()
 
-    def forward(self):
-        for k in range(3):
+    def forward(self, keys=(0, 1, 2)):
+        for k in keys:
             self.recv(k)
             self.copy(k + 6).start()
 
@@ -122,17 +145,17 @@
         return at(c + ((p + 1) % 4 - p) * stride), at(c + ((p + 3) % 4 - p) * stride)
 
     (xr, xl), (ar, al), (br, bl) = near(x, 1), near(pa, sa), near(pb, sb)
+    xo = at(c + (x + 2) % 4 - x)
     ypair = at(c + 4 - 8 * yp)
     peers = [at(c - d + (d + k) % GROUP) for k in range(1, GROUP)]
 
     def down_copies(k):
-        src = dyn(k, BLK)
-        side, dst = k // N_SIDE, dyn(k % N_SIDE, BLK)
+        src, dst, slot = pl.ds(2 * k, 2), pl.ds(2 * (k % 4), 2), 2 * (k // 4)
         q0 = pl.multiple_of(m * QH, LANES)
         return (
-            pltpu.make_async_copy(wdq.at[src, pl.ds(q0, BLK)], wbuf.at[2 * side, dst], dsem.at[0, k]),
-            pltpu.make_async_copy(wdq.at[src, pl.ds(pl.multiple_of(q0 + BLK, LANES), QB)], wbuf.at[2 * side + 1, dst, pl.ds(0, QB)], dsem.at[1, k]),
-            pltpu.make_async_copy(wdkv.at[src, dyn(m, KH)], wbuf.at[2 * side + 1, dst, pl.ds(QB, KH)], dsem.at[2, k]),
+            pltpu.make_async_copy(wdq.at[src, :, pl.ds(q0, BLK)], wbuf.at[slot, dst], dsem.at[0, k]),
+            pltpu.make_async_copy(wdq.at[src, :, pl.ds(pl.multiple_of(q0 + BLK, LANES), QB)], wbuf.at[slot + 1, dst, :, pl.ds(0, QB)], dsem.at[1, k]),
+            pltpu.make_async_copy(wdkv.at[src, :, dyn(m, KH)], wbuf.at[slot + 1, dst, :, pl.ds(QB, KH)], dsem.at[2, k]),
         )
 
     def start_down(k, _):
@@ -140,8 +163,9 @@
             cp.start()
         return 0
 
-    def out_copy(j):
-        return pltpu.make_async_copy(wout.at[:, dyn(j, BLK)], wbuf.at[lax.rem(j, N_SLOTS)], osem.at[lax.rem(j, N_SLOTS)])
+    def out_copy(t):
+        slot = lax.rem(t, N_SLOTS)
+        return pltpu.make_async_copy(wout.at[:, t // N_OUT, :, dyn(lax.rem(t, N_OUT), BLK)], wbuf.at[slot], osem.at[slot])
 
     ins = [
         pltpu.make_async_copy(a, b, isem.at[i])
@@ -153,10 +177,6 @@
     for cp in ins[:2]:
         cp.start()
     lax.fori_loop(0, N_DOWN, start_down, 0)
-    for cp in ins[2:]:
-        cp.start()
-    for j in range(N_EARLY, N_SLOTS):
-        out_copy(j).start()
 
     sem = pltpu.get_barrier_semaphore()
     greet = peers + [ar, al, br, bl, sib]
@@ -182,15 +202,17 @@
     def down(k, _):
         for cp in down_copies(k):
             cp.wait()
-        side, rows = k // N_SIDE, dyn(k % N_SIDE, BLK)
+        slot, rows = 2 * (k // 4), pl.ds(2 * (k % 4), 2)
         xb = x_v[:, dyn(k, BLK)]
-        h0[...] += dot(xb, wbuf[2 * side, rows])
-        h1[...] += dot(xb, wbuf[2 * side + 1, rows])
+        h0[...] += dot(xb, wbuf[slot, rows].reshape(BLK, BLK))
+        h1[...] += dot(xb, wbuf[slot + 1, rows].reshape(BLK, BLK))
         hkr[...] += dot_dims(xb, wkr_v[:, dyn(k, BLK)], 1, 1)
         return 0
 
     lax.fori_loop(0, N_DOWN, down, 0)
-    for j in range(N_EARLY):
+    for cp in ins[2:]:
+        cp.start()
+    for j in range(N_SLOTS):
         out_copy(j).start()
 
     h_q = jnp.concatenate([h0[...], h1[:, :QB]], axis=-1)
@@ -225,7 +247,7 @@
     def row_ring(b, row):
         return Ring(lambda p, h: lat.at[m, h, p, b], lambda p: kr.at[m, p, b], pa, ar, al, ssem, rsem, row)
 
-    r1 = Ring(lambda p, h: lat.at[m, h, pa, pb, p], lambda p: kr.at[m, pa, pb, p], x, xr, xl, ssem, rsem, 0)
+    r1 = Direct(lambda p, h: lat.at[m, h, pa, pb, p], lambda p: kr.at[m, pa, pb, p], x, (xr, xl, xo), ssem, rsem, 0)
     r2 = Ring(lambda p, h: lat.at[m, h, pa, p], lambda p: kr.at[m, pa, p], pb, br, bl, ssem, rsem, 1)
     rq = Ring(lambda p, h: cq.at[m, h, :, p], lambda p: pt.at[m, :, p], x, xr, xl, ssem, rsem, 2)
     r3 = [row_ring((pb + k) % 4, 3 + k) for k in range(4)]
@@ -237,48 +259,56 @@
             for i, ref in enumerate((cq.at[m, :, par, x], pt.at[m, par, x]))
         ]
 
-    def shares(core, planes):
-        refs = [cq.at[core], pt.at[core]]
-        for p in planes:
-            refs += [lat.at[core, :, p], kr.at[core, p]]
+    def shares(core, own, planes, rows):
+        refs = [cq.at[core], pt.at[core], lat.at[core, :, own], kr.at[core, own]]
+        for b in rows:
+            for p in planes:
+                refs += [lat.at[core, :, p, b], kr.at[core, p, b]]
         return [share(ref, k) for k, ref in enumerate(refs)]
 
-    mine = shares(m, (pa, prev, nxt, opp))
+    mine = shares(m, pa, (prev, nxt, opp), [(pb + k) % 4 for k in range(4)])
+
+    def start_shares(first_k, count):
+        for cp in mine[first_k:first_k + count]:
+            cp.start()
+
+    def row_near(k):
+        r3[k].forward()
+        r3[k].recv_near()
+        start_shares(4 + 6 * k, 4)
+
+    def row_far(k):
+        r3[k].recv_far()
+        start_shares(8 + 6 * k, 2)
 
     r1.start_own()
     for cp in pair_copies(yp):
         cp.start()
-    r1.forward()
-    r1.recv_near()
-    r1.recv_far()
+    r1.recv_all()
     r2.start_own()
-    r3[0].start_own()
     for cp in pair_copies(1 - yp):
         cp.wait_recv()
     rq.start_own()
-    r2.forward()
+    r2.forward((0,))
+    r3[0].start_own()
+    r2.forward((1, 2))
     r2.recv_near()
     r3[1].start_own()
     r3[3].start_own()
-    r3[0].forward()
-    rq.forward()
+    row_near(0)
     r2.recv_far()
     r3[2].start_own()
-    for cp in mine[2:4]:
-        cp.start()
+    start_shares(2, 2)
+    rq.forward()
+    row_near(1)
+    row_near(3)
     rq.recv_near()
     rq.recv_far()
-    for cp in mine[:2]:
-        cp.start()
-    r3[1].forward()
-    r3[3].forward()
-    r3[2].forward()
-    for r in r3:
-        r.recv_near()
-    for cp in mine[4:8]:
-        cp.start()
-
-    theirs = shares(1 - m, (0, 0, 0, 0))
+    start_shares(0, 2)
+    row_near(2)
+    row_far(0)
+
+    theirs = shares(1 - m, 0, (0, 0, 0), range(4))
     for cp in theirs[:2]:
         cp.wait_recv()
     for cp in ins[2:4]:
@@ -312,10 +342,8 @@
             qt[2 * p + a, :LANES, :] = qn_t[LANES * a:LANES * a + LANES]
             qt[2 * p + a, LANES:QK_DIM, :] = qr_t[TOK * a:TOK * a + TOK]
 
-    for r in r3:
-        r.recv_far()
-    for cp in mine[8:]:
-        cp.start()
+    for k in (1, 3, 2):
+        row_far(k)
     for cp in ins[4:]:
         cp.wait()
     for cp in theirs[2:]:
@@ -342,7 +370,7 @@
     def attn_sends(p):
         return [
             pltpu.make_async_remote_copy(
-                o_v.at[:, (d + k) % GROUP, :, dyn(p, QB)], og.at[:, :, dyn(2 * d + p, QB)],
+                o_v.at[p, :, (d + k) % GROUP], og.at[p, :, :, dyn(d, QB)],
                 assem.at[p, k - 1], arsem.at[p, k - 1], device_id=peers[k - 1], device_id_type=MESH)
             for k in range(1, GROUP)
         ]
@@ -351,17 +379,17 @@
         pc = dyn(p, QB)
 
         def up(i, _):
-            half, zz = i // 4, i % 4
-            a0 = lat[0, half, zz].reshape(BLK, KH)
-            a1 = lat[1, half, :, zz].reshape(BLK, KH)
-            rows = dyn(i, BLK)
+            half, zz = i // 2, 2 * (i % 2)
+            a0 = lat[0, half, pl.ds(zz, 2)].reshape(2 * BLK, KH)
+            a1 = jnp.concatenate([lat[1, half, :, zz + k].reshape(BLK, KH) for k in range(2)], axis=0)
+            rows = pl.ds(pl.multiple_of(i * 2 * BLK, BLK), 2 * BLK)
             kn = (dot(a0, uk_v[:KH, pc]) + dot(a1, uk_v[KH:, pc])).astype(BF)
             kcat[0, rows, :LANES] = kn[:, :LANES]
             kcat[1, rows, :LANES] = kn[:, LANES:]
             vbuf[rows, :] = (dot(a0, uv_v[:KH, pc]) + dot(a1, uv_v[KH:, pc])).astype(BF)
             return 0
 
-        lax.fori_loop(0, 8, up, 0)
+        lax.fori_loop(0, 4, up, 0)
         m_s[...] = jnp.full(m_s.shape, NEG_BIG, F32)
         l_s[...] = jnp.zeros_like(l_s)
         acc_s[...] = jnp.zeros_like(acc_s)
@@ -404,46 +432,59 @@
         for a in range(2):
             for qb in range(2):
                 ot = acc_s[a, qb] / l_s[a, qb, :1, :]
-                o_v[qb, :, :, dyn(2 * p + a, LANES)] = jnp.transpose(ot).astype(BF).reshape(GROUP, SPAN, LANES)
+                o_v[p, qb, :, :, LANES * a:LANES * a + LANES] = jnp.transpose(ot).astype(BF).reshape(GROUP, SPAN, LANES)
         for cp in attn_sends(p):
             cp.start()
+        og[p, :, :, dyn(d, QB)] = o_v[p, :, d]
         return 0
 
     lax.fori_loop(0, 2, pair, 0)
-    og[:, :, dyn(d, BLK)] = o_v[:, d]
 
     for r in [r1, r2, rq] + r3:
         r.wait_sends()
     for cp in pair_copies(yp) + mine:
         cp.wait_send()
-    for p in range(2):
-        for cp in attn_sends(p):
-            cp.wait()
+    for cp in attn_sends(0):
+        cp.wait()
 
     def y_copy(j):
         return pltpu.make_async_remote_copy(ysend.at[j], yrecv.at[j], yssem.at[j], yrsem.at[j], device_id=sib, device_id_type=MESH)
 
     def finish(j):
         y_copy(j).wait()
-        y_ref[:, dyn(j, BLK)] = (ykeep[j] + yrecv[j]).astype(BF)
-
-    def out_step(j, _):
-        out_copy(j).wait()
-        acc = dot(og[...].reshape(TOK, KEYS), wbuf[lax.rem(j, N_SLOTS)])
-        ykeep[j] = jnp.where(first, acc[:SPAN], acc[SPAN:])
+        y_ref[:, dyn(j, BLK)] = (ykeep[j, :SPAN] + yrecv[j]).astype(BF)
+
+    def half_dot(t):
+        out_copy(t).wait()
+        return dot(og[t // N_OUT].reshape(TOK, ROWS_H), wbuf[lax.rem(t, N_SLOTS)].reshape(ROWS_H, BLK))
+
+    def refill(t):
+        @pl.when(t + N_SLOTS < 2 * N_OUT)
+        def _():
+            out_copy(t + N_SLOTS).start()
+
+    def first_half(j, _):
+        ykeep[j] = half_dot(j)
+        refill(j)
+        return 0
+
+    lax.fori_loop(0, N_OUT, first_half, 0)
+    for cp in attn_sends(1):
+        cp.wait()
+
+    def second_half(j, _):
+        acc = ykeep[j] + half_dot(j + N_OUT)
+        ykeep[j, :SPAN] = jnp.where(first, acc[:SPAN], acc[SPAN:])
         ysend[j] = jnp.where(first, acc[SPAN:], acc[:SPAN])
         y_copy(j).start()
-
-        @pl.when(j + N_SLOTS < N_OUT)
-        def _():
-            out_copy(j + N_SLOTS).start()
+        refill(j + N_OUT)
 
         @pl.when(j > 0)
         def _():
             finish(j - 1)
         return 0
 
-    lax.fori_loop(0, N_OUT, out_step, 0)
+    lax.fori_loop(0, N_OUT, second_half, 0)
     finish(N_OUT - 1)
 
 
@@ -460,13 +501,13 @@
         in_specs=[hbm, vm, vm, hbm, hbm, hbm, vm, vm] + [hbm] * 5,
         out_specs=vm,
         scratch_shapes=[
-            v((TOK, HIDDEN), BF), v((TOK, HIDDEN), BF), v((N_SLOTS, KEYS, BLK), BF),
+            v((TOK, HIDDEN), BF), v((TOK, HIDDEN), BF), v((N_SLOTS, GROUP, QB, BLK), BF),
             v((TOK, BLK), F32), v((TOK, BLK), F32), v((TOK, TOK), F32), v((TOK, LANES), F32), v((TOK, LANES), F32), v((TOK, LANES), F32),
             v((2, 2, 2, 4, SPAN, QH), BF), v((2, 2, 4, 4, 4, SPAN, KH), BF), v((2, 4, 4, 4, HALF_SPAN, LANES), BF), v((2, 2, 4, HALF_SPAN, LANES), F32),
             v((Q_RANK, BLK), BF), v((Q_RANK, QB), BF), v((KV_RANK, BLK), BF), v((KV_RANK, BLK), BF),
             v((2, KEYS, QB), BF), v((KEYS, QB), BF), v((4, QK_DIM, BLK), BF), v((2, BLK, QB), F32),
-            state, state, v((2, 2, LANES, QB), F32), v((2, GROUP, SPAN, BLK), BF), v((2, SPAN, KEYS), BF), part, part, part,
-            dma((3, N_DOWN)), dma((6,)), dma((N_SLOTS,)), dma((7, 9)), dma((7, 9)), dma((10,)), dma((10,)), dma((6,)),
+            state, state, v((2, 2, LANES, QB), F32), v((2, 2, GROUP, SPAN, QB), BF), v((2, 2, SPAN, ROWS_H), BF), part, v((N_OUT, TOK, BLK), F32), part,
+            dma((3, N_DOWN)), dma((6,)), dma((N_SLOTS,)), dma((7, 9)), dma((7, 9)), dma((28,)), dma((28,)), dma((6,)),
             dma((2, 7)), dma((2, 7)), dma((N_OUT,)), dma((N_OUT,)),
         ],
         compiler_params=pltpu.CompilerParams(collective_id=0, has_side_effects=True, vmem_limit_bytes=LIMIT),
@@ -478,7 +519,7 @@
     inv = np.repeat(freq.astype(np.float32)[:, None], TOK, axis=1)
 
     def local(x_tokens, positions, w_dq, gain_q, w_uq, w_qr, w_dkv, gain_kv, w_kr, w_uk, w_uv, w_out):
-        return fused(x_tokens, positions[None], inv, w_dq, w_dkv, w_kr.T, gain_q.reshape(-1, LANES), gain_kv.reshape(-1, LANES), w_uq, w_qr, w_uk, w_uv, w_out)
+        return fused(x_tokens, positions[None], inv, w_dq.reshape(-1, QB, Q_RANK), w_dkv.reshape(-1, QB, KV_RANK), w_kr.T, gain_q.reshape(-1, LANES), gain_kv.reshape(-1, LANES), w_uq, w_qr, w_uk, w_uv, w_out.reshape(GROUP, 2, QB, HIDDEN))
 
     in_specs = (P(('dp', 'ctx'), None), P(('dp', 'ctx')), P(), P(), P(None, 'model'), P(None, 'model'), P(), P(), P(), P(None, 'model'), P(None, 'model'), P('model', None))
     out_specs = P(('dp', 'ctx', 'model'), None)

time: 79.8 us -> 77.4 us (0.970)
  Pallas kernels: 77.8 us -> 75.4 us
    pallas_call x1, Pallas kernels: 77.8 us -> 75.4 us  [fused(): pl.pallas_call(kernel, name='mla_prefill', out_shape=jax.ShapeDtypeStruct...]
where the time goes in v2:
time: 77.4 us; the launch traced here: 77.2 us
  Pallas kernels  75.4 us (97%)
  local copies, waits for them, and re-layouts  1.82 us (2%)
    pallas_call x1, Pallas kernels, fused(): pl.pallas_call(kernel, name='mla_prefill', out_shape=jax.ShapeDtypeStruct...  75.4 us
    unnamed x1, local copies, waits for them, and re-layouts  1.82 us

profile of v2, /device:TPU:1, one launch (start us, length us, event | category | flops | bytes accessed | tf_op | source)
XLA Modules:
  0.0 77.2 jit_solution(592458704559308461)
XLA Ops:
  0.0 75.4 %mla_prefill.1 = bf16[32,7168]{1,0:T(8,128)(2,1)} custom-call(bf16[64,7168]{1,0:T(8,128)(2,1)} %x_h.1, s32[1,64]{1,0:T(1,128)} %bitcast.13, f32[32,64]{1,0:T(8,128)} %constant.2.clone.inv, bf16[28,256,1536]{2,1,0:T(8,128)(2,1)} %bitcast.8, bf16[28,256,512]{2,1,0:T(8,128)(2,1)} %bitcast.9, bf16[64,7168]{1,0:T(8,128)(2,1)} %bitcast.10, f32[12,128]{1,0:T(8,128)} %bitcast.11, ...), custom_call_target="tpu_custom_call" | custom-call | tf_op jit(solution)/shard_map/mla_prefill/pallas_call | solution.py:497
  75.4 1.8 %copy.15 = bf16[32,7168]{1,0:T(8,128)(2,1)} copy(bf16[32,7168]{1,0:T(8,128)(2,1)} %mla_prefill.1) | data formatting | bytes 917504

commit v3 on v2

--- a/solution.py
+++ b/solution.py
@@ -32,6 +32,7 @@
 N_DOWN = HIDDEN // BLK
 N_OUT = HIDDEN // BLK
 N_SLOTS = 16
+LAG = 3
 N_TILES = 9
 GROUP = 8
 EXP_SCALE = QK_DIM ** -0.5 * math.log2(math.e)
@@ -124,10 +125,10 @@
             self.copy(k).wait_send()
 
 
-def kernel(x_h, pos, inv, wdq, wdkv, wkr, gq, gkv, wuq, wqr, wuk, wuv, wout, y_ref,
+def kernel(x_h, pos, inv, wdq, wdkv, wkr, gq, gkv, wuq, wqr, wuk, wuv, wout, y_h,
            x_v, wkr_v, wbuf, h0, h1, hkr, tabs, stat, stat_rx, cq, lat, kr, pt,
-           uq_v, qr_v, uk_v, uv_v, kcat, vbuf, qt, s_buf, m_s, l_s, acc_s, o_v, og, ysend, ykeep, yrecv,
-           dsem, isem, osem, ssem, rsem, dssem, drsem, psem, assem, arsem, yssem, yrsem):
+           uq_v, qr_v, uk_v, uv_v, kcat, vbuf, qt, s_buf, m_s, l_s, acc_s, o_v, og, ysend, ykeep, yrecv, y_v,
+           dsem, isem, osem, ssem, rsem, dssem, drsem, psem, assem, arsem, yssem, yrsem, ysem):
     c = lax.axis_index("ctx")
     m = lax.axis_index("model")
     x, y, z = c % 4, (c // 4) % 4, c // 16
@@ -295,11 +296,11 @@
     r2.recv_near()
     r3[1].start_own()
     r3[3].start_own()
-    row_near(0)
     r2.recv_far()
     r3[2].start_own()
     start_shares(2, 2)
     rq.forward()
+    row_near(0)
     row_near(1)
     row_near(3)
     rq.recv_near()
@@ -341,9 +342,9 @@
         for a in range(2):
             qt[2 * p + a, :LANES, :] = qn_t[LANES * a:LANES * a + LANES]
             qt[2 * p + a, LANES:QK_DIM, :] = qr_t[TOK * a:TOK * a + TOK]
-
-    for k in (1, 3, 2):
-        row_far(k)
+        for k in ((1, 3), (2,))[p]:
+            row_far(k)
+
     for cp in ins[4:]:
         cp.wait()
     for cp in theirs[2:]:
@@ -379,17 +380,16 @@
         pc = dyn(p, QB)
 
         def up(i, _):
-            half, zz = i // 2, 2 * (i % 2)
-            a0 = lat[0, half, pl.ds(zz, 2)].reshape(2 * BLK, KH)
-            a1 = jnp.concatenate([lat[1, half, :, zz + k].reshape(BLK, KH) for k in range(2)], axis=0)
-            rows = pl.ds(pl.multiple_of(i * 2 * BLK, BLK), 2 * BLK)
+            a0 = lat[0, i].reshape(ROWS_H, KH)
+            a1 = jnp.concatenate([lat[1, i, :, k].reshape(BLK, KH) for k in range(4)], axis=0)
+            rows = pl.ds(pl.multiple_of(i * ROWS_H, BLK), ROWS_H)
             kn = (dot(a0, uk_v[:KH, pc]) + dot(a1, uk_v[KH:, pc])).astype(BF)
             kcat[0, rows, :LANES] = kn[:, :LANES]
             kcat[1, rows, :LANES] = kn[:, LANES:]
             vbuf[rows, :] = (dot(a0, uv_v[:KH, pc]) + dot(a1, uv_v[KH:, pc])).astype(BF)
             return 0
 
-        lax.fori_loop(0, 4, up, 0)
+        lax.fori_loop(0, 2, up, 0)
         m_s[...] = jnp.full(m_s.shape, NEG_BIG, F32)
         l_s[...] = jnp.zeros_like(l_s)
         acc_s[...] = jnp.zeros_like(acc_s)
@@ -450,9 +450,13 @@
     def y_copy(j):
         return pltpu.make_async_remote_copy(ysend.at[j], yrecv.at[j], yssem.at[j], yrsem.at[j], device_id=sib, device_id_type=MESH)
 
+    def y_out(j):
+        return pltpu.make_async_copy(y_v.at[j], y_h.at[:, dyn(j, BLK)], ysem.at[j])
+
     def finish(j):
         y_copy(j).wait()
-        y_ref[:, dyn(j, BLK)] = (ykeep[j, :SPAN] + yrecv[j]).astype(BF)
+        y_v[j] = (ykeep[j, :SPAN] + yrecv[j]).astype(BF)
+        y_out(j).start()
 
     def half_dot(t):
         out_copy(t).wait()
@@ -479,13 +483,20 @@
         y_copy(j).start()
         refill(j + N_OUT)
 
-        @pl.when(j > 0)
+        @pl.when(j >= LAG)
         def _():
-            finish(j - 1)
+            finish(j - LAG)
         return 0
 
     lax.fori_loop(0, N_OUT, second_half, 0)
-    finish(N_OUT - 1)
+    for j in range(N_OUT - LAG, N_OUT):
+        finish(j)
+
+    def drain(j, _):
+        y_out(j).wait()
+        return 0
+
+    lax.fori_loop(0, N_OUT, drain, 0)
 
 
 def fused(x, pos, inv, wdq, wdkv, wkr, gq, gkv, wuq, wqr, wuk, wuv, wout):
@@ -499,16 +510,16 @@
         name="mla_prefill",
         out_shape=jax.ShapeDtypeStruct((SPAN, HIDDEN), BF),
         in_specs=[hbm, vm, vm, hbm, hbm, hbm, vm, vm] + [hbm] * 5,
-        out_specs=vm,
+        out_specs=hbm,
         scratch_shapes=[
             v((TOK, HIDDEN), BF), v((TOK, HIDDEN), BF), v((N_SLOTS, GROUP, QB, BLK), BF),
             v((TOK, BLK), F32), v((TOK, BLK), F32), v((TOK, TOK), F32), v((TOK, LANES), F32), v((TOK, LANES), F32), v((TOK, LANES), F32),
             v((2, 2, 2, 4, SPAN, QH), BF), v((2, 2, 4, 4, 4, SPAN, KH), BF), v((2, 4, 4, 4, HALF_SPAN, LANES), BF), v((2, 2, 4, HALF_SPAN, LANES), F32),
             v((Q_RANK, BLK), BF), v((Q_RANK, QB), BF), v((KV_RANK, BLK), BF), v((KV_RANK, BLK), BF),
             v((2, KEYS, QB), BF), v((KEYS, QB), BF), v((4, QK_DIM, BLK), BF), v((2, BLK, QB), F32),
-            state, state, v((2, 2, LANES, QB), F32), v((2, 2, GROUP, SPAN, QB), BF), v((2, 2, SPAN, ROWS_H), BF), part, v((N_OUT, TOK, BLK), F32), part,
+            state, state, v((2, 2, LANES, QB), F32), v((2, 2, GROUP, SPAN, QB), BF), v((2, 2, SPAN, ROWS_H), BF), part, v((N_OUT, TOK, BLK), F32), part, v((N_OUT, SPAN, BLK), BF),
             dma((3, N_DOWN)), dma((6,)), dma((N_SLOTS,)), dma((7, 9)), dma((7, 9)), dma((28,)), dma((28,)), dma((6,)),
-            dma((2, 7)), dma((2, 7)), dma((N_OUT,)), dma((N_OUT,)),
+            dma((2, 7)), dma((2, 7)), dma((N_OUT,)), dma((N_OUT,)), dma((N_OUT,)),
         ],
         compiler_params=pltpu.CompilerParams(collective_id=0, has_side_effects=True, vmem_limit_bytes=LIMIT),
     )(x, pos, inv, wdq, wdkv, wkr, gq, gkv, wuq, wqr, wuk, wuv, wout)

time: 77.4 us -> 74 us (0.956)
  Pallas kernels: 75.4 us -> 72 us
    pallas_call x1, Pallas kernels: 75.4 us -> 72 us  [fused(): pl.pallas_call(kernel, name='mla_prefill', out_shape=jax.ShapeDtypeStruct...]
where the time goes in v3:
time: 74 us; the launch traced here: 73.8 us
  Pallas kernels  72 us (97%)
  local copies, waits for them, and re-layouts  1.82 us (2%)
    pallas_call x1, Pallas kernels, fused(): pl.pallas_call(kernel, name='mla_prefill', out_shape=jax.ShapeDtypeStruct...  72 us
    unnamed x1, local copies, waits for them, and re-layouts  1.82 us

profile of v3, /device:TPU:1, one launch (start us, length us, event | category | flops | bytes accessed | tf_op | source)
XLA Modules:
  0.0 73.8 jit_solution(14503746173605290510)
XLA Ops:
  0.0 72.0 %mla_prefill.1 = bf16[32,7168]{1,0:T(8,128)(2,1)} custom-call(bf16[64,7168]{1,0:T(8,128)(2,1)} %x_h.1, s32[1,64]{1,0:T(1,128)} %bitcast.13, f32[32,64]{1,0:T(8,128)} %constant.2.clone.inv, bf16[28,256,1536]{2,1,0:T(8,128)(2,1)} %bitcast.8, bf16[28,256,512]{2,1,0:T(8,128)(2,1)} %bitcast.9, bf16[64,7168]{1,0:T(8,128)(2,1)} %bitcast.10, f32[12,128]{1,0:T(8,128)} %bitcast.11, ...), custom_call_target="tpu_custom_call" | custom-call | tf_op jit(solution)/shard_map/mla_prefill/pallas_call | solution.py:508
  72.0 1.8 %copy.15 = bf16[32,7168]{1,0:T(8,128)(2,1)} copy(bf16[32,7168]{1,0:T(8,128)(2,1)} %mla_prefill.1) | data formatting | bytes 917504

commit v4 on v3

--- a/solution.py
+++ b/solution.py
@@ -301,13 +301,11 @@
     start_shares(2, 2)
     rq.forward()
     row_near(0)
-    row_near(1)
-    row_near(3)
     rq.recv_near()
     rq.recv_far()
     start_shares(0, 2)
-    row_near(2)
-    row_far(0)
+    row_near(1)
+    row_near(3)
 
     theirs = shares(1 - m, 0, (0, 0, 0), range(4))
     for cp in theirs[:2]:
@@ -331,8 +329,9 @@
     cos_t = both(0)
     sin_t = both(LANES - SPAN)
     sin_t = jnp.where(lower, -sin_t, sin_t)
-    c0, c1 = cq[0].reshape(BLK, QH), cq[1].reshape(BLK, QH)
-    for p in range(2):
+
+    def queries(p):
+        c0, c1 = cq[0].reshape(BLK, QH), cq[1].reshape(BLK, QH)
         wide, thin = slice(QB * p, QB * p + QB), slice(LANES * p, LANES * p + LANES)
         qn = dot(c0, uq_v[:QH, wide]) + dot(c1, uq_v[QH:, wide])
         qr = dot(c0, qr_v[:QH, thin]) + dot(c1, qr_v[QH:, thin])
@@ -342,8 +341,13 @@
         for a in range(2):
             qt[2 * p + a, :LANES, :] = qn_t[LANES * a:LANES * a + LANES]
             qt[2 * p + a, LANES:QK_DIM, :] = qr_t[TOK * a:TOK * a + TOK]
-        for k in ((1, 3), (2,))[p]:
-            row_far(k)
+
+    queries(0)
+    row_near(2)
+    for k in (0, 1, 3):
+        row_far(k)
+    queries(1)
+    row_far(2)
 
     for cp in ins[4:]:
         cp.wait()

time: 74 us -> 74.7 us (level)
  no operation moved by 1% of the time
where the time goes in v4:
time: 74.7 us; the launch traced here: 74.5 us
  Pallas kernels  72.7 us (97%)
  local copies, waits for them, and re-layouts  1.82 us (2%)
    pallas_call x1, Pallas kernels, fused(): pl.pallas_call(kernel, name='mla_prefill', out_shape=jax.ShapeDtypeStruct...  72.7 us
    unnamed x1, local copies, waits for them, and re-layouts  1.82 us

profile of v4, /device:TPU:1, one launch (start us, length us, event | category | flops | bytes accessed | tf_op | source)
XLA Modules:
  0.0 74.5 jit_solution(13903468781672518432)
XLA Ops:
  0.0 72.7 %mla_prefill.1 = bf16[32,7168]{1,0:T(8,128)(2,1)} custom-call(bf16[64,7168]{1,0:T(8,128)(2,1)} %x_h.1, s32[1,64]{1,0:T(1,128)} %bitcast.13, f32[32,64]{1,0:T(8,128)} %constant.2.clone.inv, bf16[28,256,1536]{2,1,0:T(8,128)(2,1)} %bitcast.8, bf16[28,256,512]{2,1,0:T(8,128)(2,1)} %bitcast.9, bf16[64,7168]{1,0:T(8,128)(2,1)} %bitcast.10, f32[12,128]{1,0:T(8,128)} %bitcast.11, ...), custom_call_target="tpu_custom_call" | custom-call | tf_op jit(solution)/shard_map/mla_prefill/pallas_call | solution.py:512
  72.7 1.8 %copy.15 = bf16[32,7168]{1,0:T(8,128)(2,1)} copy(bf16[32,7168]{1,0:T(8,128)(2,1)} %mla_prefill.1) | data formatting | bytes 917504
